TPU v7x, 32 devices: a whole 2x2x4 slice. The times are simulated.
32 devices in a mesh: seq: 8 (over z, x), mp: 4 (over y, core).
Axes of the slice: x: 2, y: 2, z: 4, core: 2. Of those that a mesh axis runs over, the one named last changes fastest.
Arguments:
- grad_rows: bfloat16 [4096, 8192], P('seq', 'mp'), may hold values from -6 to 6
- img_start: int32 [64], replicated, may hold values from 0 to 4092, as said below
- img_len: int32 [64], replicated, may hold values from 4 to 64, as said below
- img_owner: int32 [64], replicated, may hold values from 0 to 7, as said below
- pre_act: bfloat16 [4096, 5120], P('seq', 'mp'), may hold values from -6 to 6
- w_out: bfloat16 [5120, 8192], P(None, 'mp'), may hold values from -0.0625 to 0.0625
Outputs:
- pre_grad: bfloat16 [4096, 5120], P('seq', 'mp')
- weight_grad: bfloat16 [5120, 8192], P('seq', 'mp')
Inputs may be any that keep to these rules, and one draw needn't show every extreme that they name: Image i lies inside positions i * 64 to (i + 1) * 64 - 1: img_start[i] - i * 64 + img_len[i] <= 64. `img_len`: A multiple of 4. In every draw some owner has all its images of exactly 64 merged tokens. `img_owner`: the images i with one value of i % 8 all have different owners, and so do the 8 images of one stripe (images i with one value of i // 8).
All inputs are finite; a program needn't handle non-finite values.
Results may differ from a plain program's by a relative error of at most 0.02.
Values may be sent and summed in bfloat16 or wider, within the bound.
A program may use at most 192 MiB of HBM per device.

v0:
```python
import math

import jax
import jax.numpy as jnp
from jax import lax
from jax.sharding import PartitionSpec as P

FRAME = 64


def gelu_parts(values):
    normal_cdf = 0.5 * (1.0 + lax.erf(values * 0.7071067811865476))
    density = jnp.exp(-0.5 * values * values) * 0.3989422804014327
    return (values * normal_cdf, normal_cdf + values * density)


def local(grad_rows, img_start, img_len, img_owner, pre_act, w_out):
    stripe = grad_rows.shape[0]
    quarter = grad_rows.shape[1]
    frames = stripe // FRAME
    owners_total = lax.axis_size("seq")
    here = lax.axis_index("seq")
    within = jnp.arange(FRAME, dtype=jnp.int32)
    first_image = here * frames
    starts = lax.dynamic_slice_in_dim(img_start, first_image, frames)
    lengths = lax.dynamic_slice_in_dim(img_len, first_image, frames)
    my_owners = lax.dynamic_slice_in_dim(img_owner, first_image, frames)
    offsets = starts - here * stripe
    row_ids = jnp.clip(offsets[:, None] + within[None, :], 0, stripe - 1)
    filled = within[None, :] < lengths[:, None]
    blocks = jnp.where(filled[:, :, None], grad_rows[row_ids], jnp.zeros((), jnp.bfloat16))
    owner_ids = jnp.arange(owners_total, dtype=jnp.int32)
    placing = (my_owners[None, :] == owner_ids[:, None]).astype(jnp.bfloat16)
    outgoing = jnp.dot(
        placing, blocks.reshape(frames, FRAME * quarter), preferred_element_type=jnp.float32
    )
    outgoing = outgoing.astype(jnp.bfloat16).reshape(owners_total * FRAME, quarter)
    received = lax.all_to_all(outgoing, "seq", split_axis=0, concat_axis=0, tiled=True)
    choosing = (img_owner.reshape(owners_total, frames) == here).T.astype(jnp.bfloat16)
    routed = jnp.dot(
        choosing,
        received.reshape(owners_total, FRAME * quarter),
        preferred_element_type=jnp.float32,
    )
    routed = routed.astype(jnp.bfloat16).reshape(stripe, quarter)
    hidden_terms = lax.dot_general(
        routed, w_out, (((1,), (1,)), ((), ())), preferred_element_type=jnp.float32
    )
    hidden_grad = lax.psum_scatter(
        hidden_terms.astype(jnp.bfloat16), "mp", scatter_dimension=1, tiled=True
    ).astype(jnp.float32)
    _, derivative = gelu_parts(pre_act.astype(jnp.float32))
    pre_grad = (hidden_grad * derivative).astype(jnp.bfloat16)
    pre_full = lax.all_gather(pre_act, "mp", axis=1, tiled=True)
    activation, _ = gelu_parts(pre_full.astype(jnp.float32))
    activation = activation.astype(jnp.bfloat16)
    factor = 1.0 / math.sqrt(owners_total * stripe)
    kept_rows = activation.shape[1] // owners_total
    act_columns = lax.all_to_all(activation, "seq", split_axis=1, concat_axis=0, tiled=True)
    shard_rows = lax.all_gather(routed, "seq", axis=0, tiled=True)
    owners_here = shard_rows.shape[0] // stripe
    product = (
        jnp.einsum(
            "kar,kaq->krq",
            act_columns.reshape(owners_here, stripe, kept_rows),
            shard_rows.reshape(owners_here, stripe, quarter),
            preferred_element_type=jnp.float32,
        )
        * factor
    )
    product = lax.optimization_barrier(product.astype(jnp.bfloat16))
    weight_grad = jnp.sum(product.astype(jnp.float32), axis=0)
    return (pre_grad, weight_grad.astype(jnp.bfloat16))


def solution(mesh):
    return jax.shard_map(
        local,
        mesh=mesh,
        in_specs=(P("seq", "mp"), P(), P(), P(), P("seq", "mp"), P(None, "mp")),
        out_specs=(P("seq", "mp"), P("seq", "mp")),
        check_vma=False,
    )
```

profile of v0, /device:TPU:8, one launch (start us, length us, event | category | flops | bytes accessed | tf_op | source)
XLA Modules:
  0.0 484.4 jit_solution(11134335510358859104)
XLA Ops:
  7.2 0.0 copy-start
  7.2 0.0 all-gather.3.cloned.1.call-start
  7.2 0.7 all-gather.3.cloned.1.call-update
  7.9 0.7 dynamic-slice_subtract_fusion
  8.7 0.1 compare_select_fusion
  8.7 0.1 reshape.100
  8.8 0.7 dynamic_slice.10
  9.5 0.0 copy-done
  9.6 3.3 gather_fusion
  12.8 0.1 iota_compare_fusion
  12.9 1.8 select_bitcast_fusion
  14.7 0.0 copy-start.5
  14.7 1.2 copy.12
  15.9 0.0 copy-done.5
  15.9 0.1 dynamic_slice.9
  16.0 0.7 convolution_convert_fusion.1
  16.7 2.5 copy.10
  19.1 6.3 %all-to-all-start = ((bf16[8,64,2048]{2,1,0:T(8,128)(2,1)}), bf16[8,64,2048]{2,1,0:T(8,128)(2,1)S(1)}, u32[]{:S(2)}, u32[]{:S(2)}) async-start(bf16[8,64,2048]{2,1,0:T(8,128)(2,1)} %copy.10), calls=%async_computation | async-start | bytes 4194304 | tf_op jit(solution)/shard_map/all_to_all | solution.py:38
  25.4 0.0 reduce-scatter.2.cloned.1.call-start
  25.4 0.1 eq.24
  25.5 45.7 %all-to-all-done = bf16[8,64,2048]{2,1,0:T(8,128)(2,1)S(1)} async-done(((bf16[8,64,2048]{2,1,0:T(8,128)(2,1)}), bf16[8,64,2048]{2,1,0:T(8,128)(2,1)S(1)}, u32[]{:S(2)}, u32[]{:S(2)}) %all-to-all-start) | async-done | bytes 2097184 | tf_op jit(solution)/shard_map/all_to_all | solution.py:38
  71.2 0.0 copy-start.3
  71.2 1.3 copy-done.3
  72.5 2.7 copy.13
  75.2 2.0 convolution_convert_fusion
  77.2 2.5 reshape.96
  79.7 0.0 copy-start.2
  79.8 17.5 %convolution_convert_fusion.2 = bf16[512,5120]{1,0:T(8,128)(2,1)} fusion(bf16[512,2048]{1,0:T(8,128)(2,1)S(1)} %reshape.96, bf16[5120,2048]{1,0:T(8,128)(2,1)} %param.11), kind=kOutput, calls=%fused_computation.10 | convolution fusion | flops 10740039680 | bytes 28311552 | tf_op jit(solution)/shard_map/dot_general | solution.py:46
  97.2 0.0 copy-done.2
  97.3 0.0 reduce-scatter.2.cloned.1.call-update
  97.3 0.0 all-gather.5.cloned.1.call-start
  97.3 0.7 all-gather.5.cloned.1.call-update
  98.0 0.0 all-gather.3.cloned.1.call-done
  98.0 6.3 %fusion.3 = bf16[512,5120]{1,0:T(8,128)(2,1)} fusion(bf16[512,5120]{1,0:T(8,128)(2,1)} %all-gather.3.cloned.1.call-done), kind=kLoop, calls=%fused_computation.9 | loop fusion | flops 15728640 | bytes 10485760 | tf_op jit(solution)/shard_map/convert_element_type | solution.py:56
  104.4 8.3 %copy.11 = bf16[512,5120]{0,1:T(8,128)(2,1)} copy(bf16[512,5120]{1,0:T(8,128)(2,1)} %fusion.3) | data formatting | bytes 10485760 | tf_op jit(solution)/shard_map/convert_element_type | solution.py:56
  112.6 0.0 copy-start.4
  112.6 6.8 %all-to-all-start.1 = ((bf16[512,8,640]{0,2,1:T(8,128)(2,1)}), bf16[512,8,640]{0,2,1:T(8,128)(2,1)}, u32[]{:S(2)}, u32[]{:S(2)}) async-start(bf16[512,8,640]{0,2,1:T(8,128)(2,1)} %bitcast.20), calls=%async_computation.2 | async-start | bytes 10485760 | tf_op jit(solution)/shard_map/all_to_all | solution.py:59
  119.5 30.1 %reduce-scatter.2.cloned.1.call-done = bf16[512,1280]{1,0:T(8,128)(2,1)} async-done(((bf16[512,5120]{1,0:T(8,128)(2,1)}), bf16[512,1280]{1,0:T(8,128)(2,1)}) %reduce-scatter.2.cloned.1.call-update) | async-done | bytes 1310736 | tf_op jit(solution)/shard_map/reduce_scatter | solution.py:49
  149.6 0.0 copy-done.4
  149.6 3.2 fusion.12
  152.8 146.9 %all-to-all-done.1 = bf16[512,8,640]{0,2,1:T(8,128)(2,1)} async-done(((bf16[512,8,640]{0,2,1:T(8,128)(2,1)}), bf16[512,8,640]{0,2,1:T(8,128)(2,1)}, u32[]{:S(2)}, u32[]{:S(2)}) %all-to-all-start.1) | async-done | bytes 5242912 | tf_op jit(solution)/shard_map/all_to_all | solution.py:59
  299.7 144.0 %all-gather.5.cloned.1.call-done = bf16[4096,2048]{1,0:T(8,128)(2,1)} async-done(((bf16[512,2048]{1,0:T(8,128)(2,1)}), bf16[4096,2048]{1,0:T(8,128)(2,1)}) %all-gather.5.cloned.1.call-update) | async-done | bytes 16777232 | tf_op jit(solution)/shard_map/all_gather | solution.py:60
  443.8 20.8 %multiply_convert_fusion = bf16[8,640,2048]{2,1,0:T(8,128)(2,1)} fusion(bf16[8,512,2048]{2,1,0:T(8,128)(2,1)} %bitcast.26, bf16[512,8,640]{0,2,1:T(8,128)(2,1)} %all-to-all-done.1), kind=kOutput, calls=%fused_computation.3 | convolution fusion | flops 10758389760 | bytes 42991616 | tf_op jit(solution)/shard_map/kar,kaq->krq/dot_general | solution.py:63
  464.5 0.0 copy-start.1
  464.6 13.4 %reduce_sum.12 = bf16[640,2048]{1,0:T(8,128)(2,1)} reduce(bf16[8,640,2048]{2,1,0:T(8,128)(2,1)} %multiply_convert_fusion, bf16[]{:T(256)} %constant.4.clone.1), dimensions={0}, to_apply=%region_1.2 | reduce | flops 9175040 | bytes 23592962 | tf_op jit(solution)/shard_map/reduce_sum | solution.py:72
  477.9 0.0 copy-done.1
  (2 shorter events, 0.0 us)
Async XLA Ops:
  7.2 2.4 copy-start
  7.2 90.9 %all-gather.3.cloned.1.call-start = ((), (), s32[]{:S(2)}) async-start(), calls=%async_computation.4 | async-start | bytes 6553600 | tf_op jit(solution)/shard_map/all_gather | solution.py:54
  14.7 1.2 copy-start.5
  19.1 52.0 %all-to-all-start = ((bf16[8,64,2048]{2,1,0:T(8,128)(2,1)}), bf16[8,64,2048]{2,1,0:T(8,128)(2,1)S(1)}, u32[]{:S(2)}, u32[]{:S(2)}) async-start(bf16[8,64,2048]{2,1,0:T(8,128)(2,1)} %copy.10), calls=%async_computation | async-start | bytes 4194304 | tf_op jit(solution)/shard_map/all_to_all | solution.py:38
  25.4 124.2 %reduce-scatter.2.cloned.1.call-start = ((), (), s32[]{:S(2)}) async-start(), calls=%async_computation.3 | async-start | bytes 6553600 | tf_op jit(solution)/shard_map/reduce_scatter | solution.py:49
  71.2 1.3 copy-start.3
  79.7 17.5 %copy-start.2 = (bf16[512,2048]{1,0:T(8,128)(2,1)}, bf16[512,2048]{1,0:T(8,128)(2,1)S(1)}, u32[]{:S(2)}) copy-start(bf16[512,2048]{1,0:T(8,128)(2,1)S(1)} %reshape.96) | copy-start | bytes 6291460
  97.3 346.5 %all-gather.5.cloned.1.call-start = ((), (), s32[]{:S(2)}) async-start(), calls=%async_computation.5 | async-start | bytes 18874368 | tf_op jit(solution)/shard_map/all_gather | solution.py:60
  112.6 37.0 %copy-start.4 = (bf16[512,1280]{1,0:T(8,128)(2,1)S(1)}, bf16[512,1280]{1,0:T(8,128)(2,1)}, u32[]{:S(2)}) copy-start(bf16[512,1280]{1,0:T(8,128)(2,1)} %param.10) | copy-start | bytes 3932164
  112.6 187.1 %all-to-all-start.1 = ((bf16[512,8,640]{0,2,1:T(8,128)(2,1)}), bf16[512,8,640]{0,2,1:T(8,128)(2,1)}, u32[]{:S(2)}, u32[]{:S(2)}) async-start(bf16[512,8,640]{0,2,1:T(8,128)(2,1)} %bitcast.20), calls=%async_computation.2 | async-start | bytes 10485760 | tf_op jit(solution)/shard_map/all_to_all | solution.py:59
  464.5 13.4 %copy-start.1 = (bf16[512,2048]{1,0:T(8,128)(2,1)S(1)}, bf16[512,2048]{1,0:T(8,128)(2,1)}, u32[]{:S(2)}) copy-start(bf16[512,2048]{1,0:T(8,128)(2,1)} %param.6) | copy-start | bytes 6291460
Sparse Core Ops, SparseCore 0:
  9.5 41.5 all-gather.2
  97.4 52.1 reduce-scatter.1
  152.3 291.3 all-gather.4
where the time goes:
time: 489 us; the launch traced here: 484 us
  waiting for transfers between devices  368 us (75%)
  matrix products  40.9 us (8%)
  other arithmetic  25.5 us (5%)
  local copies, waits for them, and re-layouts  22.8 us (5%)
  between operations  13.8 us (3%)
  starting transfers between devices  13.2 us (3%)
    all_to_all x1, waiting for transfers between devices, local(): lax.all_to_all(activation, 'seq', split_axis=1, concat_axis=0, tiled=True)  147 us
    all_gather x1, waiting for transfers between devices, local(): shard_rows = lax.all_gather(routed, 'seq', axis=0, tiled=True)  144 us
    all_to_all x1, waiting for transfers between devices, local(): lax.all_to_all(outgoing, 'seq', split_axis=0, concat_axis=0, tiled=True)  45.7 us
    reduce_scatter x1, waiting for transfers between devices, local(): lax.psum_scatter(hidden_terms.astype(jnp.bfloat16), 'mp', scatter_dimensi...  30.1 us
    dot_general x1, matrix products, local(): jnp.einsum('kar,kaq->krq', act_columns.reshape(owners_here, stripe, kept_...  20.8 us
    dot_general x1, matrix products, local(): lax.dot_general(routed, w_out, (((1,), (1,)), ((), ())), preferred_elemen...  17.5 us
    reduce_sum x1, other arithmetic, local(): weight_grad = jnp.sum(product.astype(jnp.float32), axis=0)  13.4 us
  transfers between devices with their start and end apart: 5, of which 4 were waited for; matrix products, arithmetic and copies ran while one was open for 11% of the time, Pallas kernels for 0%

commit v1 on v0

v1 whole, which is shorter than its diff:
```python
import functools
import math

import jax
import jax.numpy as jnp
from jax import lax
from jax.experimental import pallas as pl
from jax.experimental.pallas import tpu as pltpu
from jax.sharding import PartitionSpec as P

FRAME = 64
MESH = pl.DeviceIdType.MESH


def gelu_parts(values):
    normal_cdf = 0.5 * (1.0 + lax.erf(values * 0.7071067811865476))
    density = jnp.exp(-0.5 * values * values) * 0.3989422804014327
    return (values * normal_cdf, normal_cdf + values * density)


def exchange_kernel(
    n, mp, inner, pieces,
    rows_ref, act_ref, terms_ref, place_ref,
    rows_out, act_out, hid_out,
    parts, outbuf,
    rs_recv, rs_send, row_recv, row_send, act_recv, act_send, act_fwd, act_own,
    hid_recv, hid_send, local_sem,
):
    s = lax.axis_index("seq")
    m = lax.axis_index("mp")
    outer = n // inner
    z, xi = s // inner, s % inner
    stripe = rows_ref.shape[0]
    piece = stripe // pieces
    half = stripe // 2
    per = act_ref.shape[0]
    xfirst = inner == 2
    seq_peers = [((s + q) % n, m) for q in range(1, n)]
    mp_peers = [(s, (m + q) % mp) for q in range(1, mp)]

    opposite = (m + mp // 2) % mp
    greeted = seq_peers + mp_peers + [((s + q) % n, opposite) for q in range(1, n)]
    barrier = pltpu.get_barrier_semaphore()
    for peer in greeted:
        pl.semaphore_signal(barrier, inc=1, device_id=peer, device_id_type=MESH)
    pl.semaphore_wait(barrier, len(greeted))

    def remote(src, dst, send, recv, peer):
        return pltpu.make_async_remote_copy(
            src_ref=src, dst_ref=dst, send_sem=send, recv_sem=recv,
            device_id=peer, device_id_type=MESH,
        )

    def row_copy(t, p, way, peer, own=False):
        slot = rows_out.at[pl.ds(t * stripe + p * piece, piece)]
        src = rows_ref.at[pl.ds(p * piece, piece)] if own else slot
        return remote(src, slot, row_send.at[t, p, way], row_recv.at[t, p], peer)

    def go(run, copy):
        if run:
            copy.start()
        else:
            copy.wait_send()

    def arrive(run, t, p):
        if run:
            row_copy(t, p, 0, ((s + 1) % n, m)).wait_recv()

    def up(run, t, p, own=False):
        @pl.when(z < outer - 1)
        def _():
            go(run, row_copy(t, p, 0, (s + inner, m), own))

    def down(run, t, p, own=False):
        @pl.when(z > 0)
        def _():
            go(run, row_copy(t, p, 1, (s - inner, m), own))

    def across(run, t, p, own=False):
        for q in range(1, inner):
            go(run, row_copy(t, p, 1 + q, (z * inner + (xi + q) % inner, m), own))

    def loop(first, body):
        def step(p, carry):
            body(p)
            return carry
        lax.fori_loop(first, pieces, step, 0)

    def own_rows(run):
        def body(p):
            up(run, s, p, True)
            down(run, s, p, True)
            across(run, s, p, True)
        loop(0, body)

    def partner_rows(run):
        if xfirst:
            t = z * inner + (1 - xi)
            arrive(run, t, 0)
            up(run, t, 0)
            down(run, t, 0)

    def hop(run, d):
        def one(p, crossing):
            @pl.when(z >= d)
            def _():
                t = s - d * inner
                arrive(run, t, p)
                up(run, t, p)
                if crossing:
                    across(run, t, p)
                else:
                    t2 = (z - d) * inner + (1 - xi)
                    arrive(run, t2, p)
                    up(run, t2, p)

            @pl.when(z + d < outer)
            def _():
                t = s + d * inner
                arrive(run, t, p)
                down(run, t, p)
                if crossing:
                    across(run, t, p)
                else:
                    t2 = (z + d) * inner + (1 - xi)
                    arrive(run, t2, p)
                    down(run, t2, p)

        if xfirst:
            one(0, False)
            loop(1, lambda p: one(p, True))
        else:
            loop(0, lambda p: one(p, True))

    def rest_rows():
        for zz in range(outer):
            for q in range(1, inner):
                t = zz * inner + (xi + q) % inner
                loop(1 if xfirst else 0, lambda p: arrive(True, t, p))

    root_a = s // per
    root_b = (root_a + mp // 2) % mp

    def act_slot(t, h):
        return act_out.at[pl.ds(t * stripe + h * half, half)]

    def act_first(run):
        for j in range(per):
            target = m * per + j

            @pl.when(target != s)
            def _():
                for h, to in ((0, m), (1, opposite)):
                    go(run, remote(
                        act_ref.at[j, pl.ds(h * half, half)], act_slot(s, h),
                        act_send.at[j, h], act_recv.at[s, h], (target, to),
                    ))

            @pl.when(target == s)
            def _():
                for h in range(2):
                    for q, peer in enumerate(mp_peers):
                        go(run, remote(
                            act_ref.at[j, pl.ds(h * half, half)], act_slot(s, h),
                            act_own.at[h, q], act_recv.at[s, h], peer,
                        ))
                mine = pltpu.make_async_copy(
                    act_ref.at[j], act_out.at[pl.ds(s * stripe, stripe)], local_sem.at[1]
                )
                if run:
                    mine.start()
                else:
                    mine.wait()

    def act_wait(t, h):
        remote(act_slot(t, h), act_slot(t, h), act_fwd.at[0, 0], act_recv.at[t, h], mp_peers[0]).wait_recv()

    def act_pass(run):
        for h, root in ((0, root_a), (1, root_b)):
            @pl.when(m == root)
            def _():
                for k in range(1, n):
                    t = (s + k) % n
                    if run:
                        act_wait(t, h)
                    for q, peer in enumerate(mp_peers):
                        go(run, remote(
                            act_slot(t, h), act_slot(t, h), act_fwd.at[t, q], act_recv.at[t, h], peer,
                        ))

    def act_rest():
        for h, root in ((0, root_a), (1, root_b)):
            @pl.when(m != root)
            def _():
                for k in range(1, n):
                    act_wait((s + k) % n, h)

            @pl.when(m != root_a)
            def _():
                act_wait(s, h)

    def sums(run):
        for q, peer in enumerate(mp_peers):
            go(run, remote(terms_ref.at[peer[1]], parts.at[m], rs_send.at[q], rs_recv.at[m], peer))

    def hid_copy(q):
        peer = ((s + q) % n, m)
        return remote(
            outbuf.at[pl.ds(pl.multiple_of(peer[0] * FRAME, FRAME), FRAME)],
            hid_out.at[pl.ds(pl.multiple_of(s * FRAME, FRAME), FRAME)],
            hid_send.at[q], hid_recv.at[s], peer,
        )

    def hid_mine():
        at = pl.ds(pl.multiple_of(s * FRAME, FRAME), FRAME)
        return pltpu.make_async_copy(outbuf.at[at], hid_out.at[at], local_sem.at[2])

    def hidden():
        for q, peer in enumerate(mp_peers):
            remote(terms_ref.at[0], parts.at[peer[1]], rs_send.at[q], rs_recv.at[peer[1]], peer).wait_recv()
        width = parts.shape[2]
        chunk = 256 if width % 256 == 0 else width

        def step(c, carry):
            at = pl.ds(pl.multiple_of(c * chunk, chunk), chunk)
            total = terms_ref[m, :, at].astype(jnp.float32)
            for q in range(1, mp):
                total = total + parts[(m + q) % mp, :, at].astype(jnp.float32)
            outbuf[:, at] = jnp.dot(
                place_ref[...], total.astype(jnp.bfloat16), preferred_element_type=jnp.float32
            ).astype(jnp.bfloat16)
            return carry

        lax.fori_loop(0, width // chunk, step, 0)

    def hid_wait(t):
        at = pl.ds(pl.multiple_of(t * FRAME, FRAME), FRAME)
        remote(outbuf.at[pl.ds(0, FRAME)], hid_out.at[at], hid_send.at[1], hid_recv.at[t], seq_peers[0]).wait_recv()

    keep = pltpu.make_async_copy(rows_ref, rows_out.at[pl.ds(s * stripe, stripe)], local_sem.at[0])
    own_rows(True)
    sums(True)
    act_first(True)
    keep.start()
    partner_rows(True)
    hop(True, 1)
    hidden()
    hop(True, 2)
    for q in range(1, n):
        hid_copy(q).start()
    hid_mine().start()
    act_pass(True)
    for d in range(3, outer):
        hop(True, d)
    rest_rows()
    act_rest()
    for q in range(1, n):
        hid_wait((s + q) % n)

    keep.wait()
    hid_mine().wait()
    own_rows(False)
    sums(False)
    act_first(False)
    partner_rows(False)
    for d in range(1, outer):
        hop(False, d)
    act_pass(False)
    for q in range(1, n):
        hid_copy(q).wait_send()


def exchange(n, mp, rows, acts, terms, place):
    stripe, quarter = rows.shape
    per, _, kept = acts.shape
    width = terms.shape[2]
    inner = n // 4
    pieces = 8 if inner == 2 else 1
    vm = pl.BlockSpec(memory_space=pltpu.VMEM)
    anywhere = pl.BlockSpec(memory_space=pl.ANY)
    dma = pltpu.SemaphoreType.DMA
    return pl.pallas_call(
        functools.partial(exchange_kernel, n, mp, inner, pieces),
        out_shape=(
            jax.ShapeDtypeStruct((n * stripe, quarter), jnp.bfloat16),
            jax.ShapeDtypeStruct((n * stripe, kept), jnp.bfloat16),
            jax.ShapeDtypeStruct((n * FRAME, width), jnp.bfloat16),
        ),
        in_specs=[vm] * 4,
        out_specs=(anywhere,) * 3,
        scratch_shapes=[
            pltpu.VMEM((mp, stripe, width), jnp.bfloat16),
            pltpu.VMEM((n * FRAME, width), jnp.bfloat16),
            dma((mp,)), dma((mp,)),
            dma((n, pieces)), dma((n, pieces, 1 + inner)),
            dma((n, 2)), dma((per, 2)), dma((n, mp)), dma((2, mp)),
            dma((n,)), dma((n,)), dma((3,)),
        ],
        compiler_params=pltpu.CompilerParams(
            collective_id=0, has_side_effects=True, vmem_limit_bytes=60 * 1024 * 1024
        ),
    )(rows, acts, terms, place)


def local(n, mp, grad_rows, img_start, img_len, img_owner, pre_act, w_out):
    stripe, quarter = grad_rows.shape
    width = pre_act.shape[1]
    kept = w_out.shape[0] // n
    frames = stripe // FRAME
    here = lax.axis_index("seq")
    owner = img_owner.reshape(n, frames)
    starts = img_start.reshape(n, frames)
    lengths = img_len.reshape(n, frames)
    row = jnp.arange(FRAME, dtype=jnp.int32)
    image = jnp.arange(n * frames, dtype=jnp.int32).reshape(n, frames)

    mine = (owner == here).astype(jnp.int32)
    offset = jnp.sum(mine * (starts - image * FRAME), axis=0)
    length = jnp.sum(mine * lengths, axis=0)
    token = row[None, :] - offset[:, None]
    token = jnp.where((token >= 0) & (token < length[:, None]), token, -1)
    block = jnp.arange(frames, dtype=jnp.int32)[:, None] * FRAME
    source = jnp.where(token >= 0, block + token, -1).reshape(stripe, 1)
    column = jnp.arange(stripe, dtype=jnp.int32)[None, :]
    shift = (source == column).astype(jnp.bfloat16)

    values = pre_act.astype(jnp.float32)
    activation, derivative = gelu_parts(values)
    activation = activation.astype(jnp.bfloat16)
    shifted = jnp.dot(shift, activation, preferred_element_type=jnp.float32).astype(jnp.bfloat16)
    acts = shifted.reshape(stripe, width // kept, kept).transpose(1, 0, 2)

    my_owner = lax.dynamic_slice_in_dim(owner, here, 1)[0]
    my_start = lax.dynamic_slice_in_dim(starts, here, 1)[0] - here * stripe
    my_length = lax.dynamic_slice_in_dim(lengths, here, 1)[0]
    to = (my_owner[None, :] == jnp.arange(n, dtype=jnp.int32)[:, None]).astype(jnp.int32)
    first = jnp.sum(to * my_start[None, :], axis=1)
    count = jnp.sum(to * my_length[None, :], axis=1)
    at = jnp.where(row[None, :] < count[:, None], first[:, None] + row[None, :], -1)
    place = (at.reshape(n * FRAME, 1) == column).astype(jnp.bfloat16)

    terms = jnp.stack([
        lax.dot_general(
            grad_rows, w_out[q * width:(q + 1) * width], (((1,), (1,)), ((), ())),
            preferred_element_type=jnp.float32,
        ).astype(jnp.bfloat16)
        for q in range(mp)
    ])

    rows_all, act_all, hid = exchange(n, mp, grad_rows, acts, terms, place)

    slot = jnp.arange(stripe, dtype=jnp.int32)
    came = jnp.arange(n * FRAME, dtype=jnp.int32)
    from_me = (owner == here).T
    pick = jnp.repeat(jnp.repeat(from_me, FRAME, axis=0), FRAME, axis=1)
    pick = (pick & (slot[:, None] % FRAME == came[None, :] % FRAME)).astype(jnp.bfloat16)
    hidden_grad = jnp.dot(pick, hid, preferred_element_type=jnp.float32)
    pre_grad = (hidden_grad * derivative).astype(jnp.bfloat16)

    order = (img_owner * frames + jnp.arange(n * frames, dtype=jnp.int32) % frames)
    act_pos = act_all.reshape(n * frames, FRAME, kept)[order].reshape(n * stripe, kept)
    factor = 1.0 / math.sqrt(n * stripe)
    weight_grad = lax.dot_general(
        act_pos, rows_all, (((0,), (0,)), ((), ())), preferred_element_type=jnp.float32
    ) * factor
    return (pre_grad, weight_grad.astype(jnp.bfloat16))


def solution(mesh):
    return jax.shard_map(
        functools.partial(local, mesh.shape["seq"], mesh.shape["mp"]),
        mesh=mesh,
        in_specs=(P("seq", "mp"), P(), P(), P(), P("seq", "mp"), P(None, "mp")),
        out_specs=(P("seq", "mp"), P("seq", "mp")),
        check_vma=False,
    )
```

time: 489 us -> 320 us (0.65)
  waiting for transfers between devices: 368 us -> 0 us
  Pallas kernels: 0 us -> 257 us
  other arithmetic: 25.5 us -> 4.61 us
  starting transfers between devices: 13.2 us -> 0 us
  between operations: 13.8 us -> 0.74 us
  local copies, waits for them, and re-layouts: 22.8 us -> 12.1 us
    pallas_call x0 -> x1, Pallas kernels: none -> 257 us  [exchange(): pl.pallas_call(functools.partial(exchange_kernel, n, mp, inner, pieces),...]
    all_to_all x2 -> x0, waiting for transfers between devices: 193 us -> none  [the longest x1 147 us: local(): lax.all_to_all(activation, 'seq', split_axis=1, concat_axis=0, tiled=True)]
    all_gather x2 -> x0, waiting for transfers between devices: 144 us -> none  [the longest x1 144 us: local(): shard_rows = lax.all_gather(routed, 'seq', axis=0, tiled=True)]
    reduce_scatter x1 -> x0, waiting for transfers between devices: 30.1 us -> none  [local(): lax.psum_scatter(hidden_terms.astype(jnp.bfloat16), 'mp', scatter_dimensi...]
    reduce_sum x1 -> x2, other arithmetic: 13.4 us -> 0.17 us  [the longest x1 0.15 us: local(): count = jnp.sum(to * my_length[None, :], axis=1)]
    all_to_all x2 -> x0, starting transfers between devices: 13.1 us -> none  [the longest x1 6.85 us: local(): lax.all_to_all(activation, 'seq', split_axis=1, concat_axis=0, tiled=True)]
    convert_element_type x2 -> x1, other arithmetic: 9.49 us -> 0.96 us  [local(): place = (at.reshape(n * FRAME, 1) == column).astype(jnp.bfloat16)]
    convert_element_type x1, local copies, waits for them, and re-layouts: 8.28 us -> 1.75 us  [local(): jnp.dot(shift, activation, preferred_element_type=jnp.float32)]
  transfers between devices with their start and end apart: 5 -> 0, of which waited for: 4 -> 0; matrix products, arithmetic and copies ran while one was open for 11% -> 0% of each run, Pallas kernels for 0% -> 0%
where the time goes in v1:
time: 320 us
  Pallas kernels  257 us (80%)
  matrix products  45.4 us (14%)
  local copies, waits for them, and re-layouts  12.1 us (4%)
  other arithmetic  4.61 us (1%)
    pallas_call x1, Pallas kernels, exchange(): pl.pallas_call(functools.partial(exchange_kernel, n, mp, inner, pieces),...  257 us
    dot_general x4, matrix products, local(): lax.dot_general(grad_rows, w_out[q * width:(q + 1) * width], (((1,), (1,)...  21.9 us
    dot_general x1, matrix products, local(): lax.dot_general(act_pos, rows_all, (((0,), (0,)), ((), ())), preferred_el...  17.4 us

profile of v1, /device:TPU:8, one launch (start us, length us, event | category | flops | bytes accessed | tf_op | source)
XLA Modules:
  0.0 319.9 jit_solution(9815206203838883249)
XLA Ops:
  0.6 0.7 reshape.143
  1.4 0.7 reshape.140
  2.1 0.7 reshape.147
  2.9 0.1 select_reduce_fusion.1
  3.0 0.1 add_select_fusion
  3.1 0.1 select_n.65
  3.2 1.0 fusion.41.place_ref
  4.1 0.1 lt.56
  4.2 0.1 lt.57
  4.3 0.1 iota_subtract_fusion
  4.4 0.1 sub.38
  4.4 0.1 add.81
  4.5 0.1 add.82
  4.6 3.5 %convolution_convert_fusion = bf16[512,1280]{1,0:T(8,128)(2,1)} fusion(bf16[512,1280]{1,0:T(8,128)(2,1)} %param.10, s32[512]{0:T(512)S(1)} %add_select_fusion.2), kind=kOutput, calls=%fused_computation.22 | convolution fusion | flops 675938304 | bytes 2623488 | tf_op jit(solution)/shard_map/dot_general | solution.py:330
  8.1 0.0 copy-start
  8.1 1.8 copy.9
  9.9 1.4 copy.10
  11.3 0.0 copy-done
  11.3 5.5 %fusion.21 = bf16[1,512,1280]{2,1,0:T(8,128)(2,1)S(1)} fusion(bf16[512,2048]{1,0:T(8,128)(2,1)S(1)} %copy-done, bf16[5120,2048]{1,0:T(8,128)(2,1)} %param.11), kind=kOutput, calls=%fused_computation.23 | convolution fusion | flops 2685009920 | bytes 8650752 | tf_op jit(solution)/shard_map/dot_general | solution.py:343
  16.8 5.5 %fusion.24 = bf16[1,512,1280]{2,1,0:T(8,128)(2,1)S(1)} fusion(bf16[512,2048]{1,0:T(8,128)(2,1)S(1)} %copy-done, bf16[5120,2048]{1,0:T(8,128)(2,1)} %param.11), kind=kOutput, calls=%fused_computation.24 | convolution fusion | flops 2685009920 | bytes 8650752 | tf_op jit(solution)/shard_map/dot_general | solution.py:343
  22.3 5.5 %fusion.27 = bf16[1,512,1280]{2,1,0:T(8,128)(2,1)S(1)} fusion(bf16[512,2048]{1,0:T(8,128)(2,1)S(1)} %copy-done, bf16[5120,2048]{1,0:T(8,128)(2,1)} %param.11), kind=kOutput, calls=%fused_computation.25 | convolution fusion | flops 2685009920 | bytes 8650752 | tf_op jit(solution)/shard_map/dot_general | solution.py:343
  27.8 5.5 %fusion.30 = bf16[1,512,1280]{2,1,0:T(8,128)(2,1)S(1)} fusion(bf16[512,2048]{1,0:T(8,128)(2,1)S(1)} %copy-done, bf16[5120,2048]{1,0:T(8,128)(2,1)} %param.11), kind=kOutput, calls=%fused_computation.26 | convolution fusion | flops 2685009920 | bytes 8650752 | tf_op jit(solution)/shard_map/dot_general | solution.py:343
  33.3 3.0 pad_maximum_fusion.terms_ref
  36.3 0.0 copy-start.1
  36.3 257.0 %shard_map.77 = (bf16[4096,2048]{1,0:T(8,128)(2,1)}, bf16[4096,640]{1,0:T(8,128)(2,1)}, bf16[512,1280]{1,0:T(8,128)(2,1)}) custom-call(bf16[512,2048]{1,0:T(8,128)(2,1)} %rows_ref.1, bf16[2,512,640]{2,1,0:T(8,128)(2,1)} %bitcast.31, bf16[4,512,1280]{2,1,0:T(8,128)(2,1)} %pad_maximum_fusion.terms_ref, bf16[512,512]{1,0:T(8,128)(2,1)} %fusion.41.place_ref), custom_call_target="tpu_custom_call" | custom-call | tf_op jit(solution)/shard_map/pallas_call | solution.py:282
  293.4 0.0 copy-done.1
  293.4 6.0 %gather_fusion = bf16[64,64,640]{2,1,0:T(8,128)(2,1)} fusion(bf16[64,64,640]{2,1,0:T(8,128)(2,1)} %bitcast.33, s32[1024]{0:T(1024)S(1)} %pad_clamp_fusion), kind=kCustom, calls=%fused_computation | custom fusion | bytes 10486016 | tf_op jit(solution)/shard_map/gather | solution.py:361
  299.4 0.0 copy-start.2
  299.4 0.0 copy-start.3
  299.4 17.4 %multiply_convert_fusion = bf16[640,2048]{1,0:T(8,128)(2,1)} fusion(bf16[4096,640]{1,0:T(8,128)(2,1)} %bitcast.34, bf16[4096,2048]{1,0:T(8,128)(2,1)} %get-tuple-element.7), kind=kOutput, calls=%fused_computation.2 | convolution fusion | flops 10740039680 | bytes 24641536 | tf_op jit(solution)/shard_map/dot_general | solution.py:363
  316.8 0.1 broadcast_in_dim.14
  316.9 0.1 reshape.141
  317.0 0.2 bitcast_and_fusion
  317.2 0.0 copy-done.2
  317.2 0.0 copy-done.3
  317.2 2.6 fusion.8
  (8 shorter events, 0.1 us)
Async XLA Ops:
  8.1 3.2 %copy-start = (bf16[512,2048]{1,0:T(8,128)(2,1)S(1)}, bf16[512,2048]{1,0:T(8,128)(2,1)}, u32[]{:S(2)}) copy-start(bf16[512,2048]{1,0:T(8,128)(2,1)} %rows_ref.1) | copy-start | bytes 6291460
  36.3 257.1 %copy-start.1 = (s32[64]{0:T(128)S(1)}, s32[64]{0:T(128)}, u32[]{:S(2)}) copy-start(s32[64]{0:T(128)} %param.9) | copy-start | bytes 772
  299.4 17.8 %copy-start.2 = (bf16[512,1280]{1,0:T(8,128)(2,1)S(1)}, bf16[512,1280]{1,0:T(8,128)(2,1)}, u32[]{:S(2)}) copy-start(bf16[512,1280]{1,0:T(8,128)(2,1)} %param.10) | copy-start | bytes 3932164
  299.4 17.8 %copy-start.3 = (bf16[512,1280]{1,0:T(8,128)(2,1)S(1)}, bf16[512,1280]{1,0:T(8,128)(2,1)}, u32[]{:S(2)}) copy-start(bf16[512,1280]{1,0:T(8,128)(2,1)} %get-tuple-element.5) | copy-start | bytes 3932164
